TPU v7x, 32 devices: a whole 2x2x4 slice. The times are simulated.
32 devices in a mesh: dp: 4 (over x, core), pipe: 2 (over y), tensor: 4 (over z).
Axes of the slice: x: 2, y: 2, z: 4, core: 2. Of those that a mesh axis runs over, the one named last changes fastest.
Arguments:
- weights: bfloat16 [2816, 1408], P(('dp', 'pipe', 'tensor')), may hold values from -6 to 6
- first_moment: bfloat16 [2816, 1408], P(('dp', 'pipe', 'tensor')), may hold values from -6 to 6
- second_moment: bfloat16 [2816, 1408], P(('dp', 'pipe', 'tensor')), may hold values from 0.049804688 to 5
- row_weight: float32 [1408], replicated, may hold values from -1 to 1
- col_weight: float32 [1408], replicated, may hold values from 1 to 4
Outputs:
- weight_tiles: bfloat16 [2816, 1408], P(('pipe', 'tensor'))
- first_tiles: bfloat16 [2816, 1408], P(('pipe', 'tensor'))
- second_tiles: bfloat16 [2816, 1408], P(('pipe', 'tensor'))
- checksums: float32 [3, 2, 4, 11], P(None, 'pipe', 'tensor')
All inputs are finite; a program needn't handle non-finite values.
Results may differ from a plain program's by a relative error of at most 0.001.
Values may be sent and summed in bfloat16 or wider, within the bound.
A program may use at most 64 MiB of HBM per device.

v0:
```python
import jax
import jax.numpy as jnp
from jax import lax
from jax.sharding import PartitionSpec as P

CHECK_COLS = 128


def for_sending(array):
    return jax.tree.map(lambda a: a.astype(jnp.bfloat16) if a.dtype == jnp.float32 else a, array)


def column_sums(data, row_part, col_weight, col_blocks):
    row_mixed = jnp.dot(
        row_part[None, :], data.astype(jnp.float32), precision=lax.Precision.HIGHEST
    )[0]
    return jnp.sum((row_mixed * col_weight).reshape(col_blocks, -1), axis=1)


def shards(weights, first_moment, second_moment, row_weight, col_weight):
    dp_count = lax.axis_size("dp")
    pipe_count = lax.axis_size("pipe")
    tensor_count = lax.axis_size("tensor")
    shard_rows, width = weights.shape
    dp_section = dp_count // pipe_count
    tile_shards = dp_count // tensor_count
    piece_cols = width // dp_count
    tile_rows = shard_rows * dp_count
    col_blocks = width // CHECK_COLS
    factor = float(tile_rows * CHECK_COLS) ** (-0.5)
    sources = (weights, first_moment, second_moment)
    exchanged = (
        lax.all_to_all(sources[0], "dp", split_axis=1, concat_axis=0, tiled=True),
        lax.all_to_all(sources[1], "dp", split_axis=1, concat_axis=0, tiled=True),
        lax.all_to_all(sources[2], "dp", split_axis=1, concat_axis=0, tiled=True),
    )
    grouped = tuple(
        (item.reshape(pipe_count, dp_section, shard_rows, piece_cols) for item in exchanged)
    )
    sectioned = jax.tree.map(
        lambda part, own: part.astype(own.dtype),
        lax.all_to_all(for_sending(grouped), "pipe", split_axis=0, concat_axis=2, tiled=True),
        grouped,
    )
    routed = tuple(
        (item.reshape(tensor_count, tile_shards, 1, shard_rows, piece_cols) for item in sectioned)
    )
    arrived = jax.tree.map(
        lambda part, own: part.astype(own.dtype),
        lax.all_to_all(for_sending(routed), "tensor", split_axis=0, concat_axis=2, tiled=True),
        routed,
    )
    flat_pieces = tuple((item.reshape(tile_rows, piece_cols) for item in arrived))
    tiles = jax.tree.map(
        lambda part, own: part.astype(own.dtype),
        lax.all_gather(for_sending(flat_pieces), "dp", axis=1, tiled=True),
        flat_pieces,
    )
    tensor_pos = lax.axis_index("tensor")
    flat_index = (
        lax.axis_index("dp") * pipe_count + lax.axis_index("pipe")
    ) * tensor_count + tensor_pos
    in_section = flat_index % (dp_count * tensor_count)
    section_of = flat_index // (dp_count * tensor_count)
    tile_of = in_section // dp_count
    row_part = lax.dynamic_slice_in_dim(row_weight, in_section * shard_rows, shard_rows)
    partial_value = jnp.stack(
        [column_sums(item, row_part, col_weight, col_blocks) for item in sources]
    )
    section_hit = (jnp.arange(pipe_count) == section_of).astype(jnp.float32)
    tile_hit = (jnp.arange(tensor_count) == tile_of).astype(jnp.float32)
    spread = (
        partial_value[:, None, None, :]
        * section_hit[None, :, None, None]
        * tile_hit[None, None, :, None]
    )
    summed = lax.psum(spread, ("dp", "pipe", "tensor"))
    checks = (
        lax.dynamic_slice(summed, (0, lax.axis_index("pipe"), tensor_pos, 0), (3, 1, 1, col_blocks))
        * factor
    )
    return (tiles[0], tiles[1], tiles[2], checks)


def solution(mesh):
    return jax.shard_map(
        shards,
        mesh=mesh,
        in_specs=(
            P(("dp", "pipe", "tensor"), None),
            P(("dp", "pipe", "tensor"), None),
            P(("dp", "pipe", "tensor"), None),
            P(),
            P(),
        ),
        out_specs=(
            P(("pipe", "tensor"), None),
            P(("pipe", "tensor"), None),
            P(("pipe", "tensor"), None),
            P(None, "pipe", "tensor", None),
        ),
        check_vma=False,
    )
```

profile of v0, /device:TPU:5, one launch (start us, length us, event | category | flops | bytes accessed | tf_op | source)
XLA Modules:
  0.0 152.4 jit_solution(8427268718347811385)
XLA Ops:
  0.7 1.3 all_to_all.90
  1.9 0.7 copy.33
  2.7 4.8 %all-to-all-start = ((bf16[88,4,352]{2,0,1:T(8,128)(2,1)}), bf16[88,4,352]{2,0,1:T(8,128)(2,1)}, u32[]{:S(2)}, u32[]{:S(2)}) async-start(bf16[88,4,352]{2,0,1:T(8,128)(2,1)} %copy.33), calls=%async_computation | async-start | bytes 540672 | tf_op jit(solution)/shard_map/all_to_all | solution.py:33
  7.8 0.7 copy.37
  8.5 4.2 %all-to-all-done = bf16[88,4,352]{2,0,1:T(8,128)(2,1)} async-done(((bf16[88,4,352]{2,0,1:T(8,128)(2,1)}), bf16[88,4,352]{2,0,1:T(8,128)(2,1)}, u32[]{:S(2)}, u32[]{:S(2)}) %all-to-all-start) | async-done | bytes 247840 | tf_op jit(solution)/shard_map/all_to_all | solution.py:33
  12.8 5.0 %all-to-all-start.3 = ((bf16[88,4,352]{2,0,1:T(8,128)(2,1)}), bf16[88,4,352]{2,0,1:T(8,128)(2,1)}, u32[]{:S(2)}, u32[]{:S(2)}) async-start(bf16[88,4,352]{2,0,1:T(8,128)(2,1)} %copy.37), calls=%async_computation.3 | async-start | bytes 540672 | tf_op jit(solution)/shard_map/all_to_all | solution.py:34
  18.1 0.7 copy.41
  18.8 4.2 %all-to-all-done.3 = bf16[88,4,352]{2,0,1:T(8,128)(2,1)} async-done(((bf16[88,4,352]{2,0,1:T(8,128)(2,1)}), bf16[88,4,352]{2,0,1:T(8,128)(2,1)}, u32[]{:S(2)}, u32[]{:S(2)}) %all-to-all-start.3) | async-done | bytes 247840 | tf_op jit(solution)/shard_map/all_to_all | solution.py:34
  23.0 5.0 %all-to-all-start.6 = ((bf16[88,4,352]{2,0,1:T(8,128)(2,1)}), bf16[88,4,352]{2,0,1:T(8,128)(2,1)}, u32[]{:S(2)}, u32[]{:S(2)}) async-start(bf16[88,4,352]{2,0,1:T(8,128)(2,1)} %copy.41), calls=%async_computation.6 | async-start | bytes 540672 | tf_op jit(solution)/shard_map/all_to_all | solution.py:35
  28.3 0.3 convolution_reduce_fusion
  28.6 4.6 %all-to-all-done.6 = bf16[88,4,352]{2,0,1:T(8,128)(2,1)} async-done(((bf16[88,4,352]{2,0,1:T(8,128)(2,1)}), bf16[88,4,352]{2,0,1:T(8,128)(2,1)}, u32[]{:S(2)}, u32[]{:S(2)}) %all-to-all-start.6) | async-done | bytes 247840 | tf_op jit(solution)/shard_map/all_to_all | solution.py:35
  33.2 3.4 %all-to-all-start.1 = ((bf16[2,2,88,352]{3,2,1,0:T(8,128)(2,1)}), bf16[2,2,88,352]{3,2,1,0:T(8,128)(2,1)S(1)}, u32[]{:S(2)}, u32[]{:S(2)}) async-start(bf16[2,2,88,352]{3,2,1,0:T(8,128)(2,1)} %bitcast.1), calls=%async_computation.1 | async-start | bytes 540672 | tf_op jit(solution)/shard_map/all_to_all | solution.py:42
  36.7 0.3 convolution_reduce_fusion.1
  37.2 2.1 %all-to-all-done.1 = bf16[2,2,88,352]{3,2,1,0:T(8,128)(2,1)S(1)} async-done(((bf16[2,2,88,352]{3,2,1,0:T(8,128)(2,1)}), bf16[2,2,88,352]{3,2,1,0:T(8,128)(2,1)S(1)}, u32[]{:S(2)}, u32[]{:S(2)}) %all-to-all-start.1) | async-done | bytes 247840 | tf_op jit(solution)/shard_map/all_to_all | solution.py:42
  39.2 5.5 %all-to-all-start.4 = ((bf16[2,2,88,352]{3,2,1,0:T(8,128)(2,1)}), bf16[2,2,88,352]{3,2,1,0:T(8,128)(2,1)S(1)}, u32[]{:S(2)}, u32[]{:S(2)}) async-start(bf16[2,2,88,352]{3,2,1,0:T(8,128)(2,1)} %bitcast.8), calls=%async_computation.4 | async-start | bytes 540672 | tf_op jit(solution)/shard_map/all_to_all | solution.py:42
  44.8 2.6 %all-to-all-done.4 = bf16[2,2,88,352]{3,2,1,0:T(8,128)(2,1)S(1)} async-done(((bf16[2,2,88,352]{3,2,1,0:T(8,128)(2,1)}), bf16[2,2,88,352]{3,2,1,0:T(8,128)(2,1)S(1)}, u32[]{:S(2)}, u32[]{:S(2)}) %all-to-all-start.4) | async-done | bytes 247840 | tf_op jit(solution)/shard_map/all_to_all | solution.py:42
  47.4 4.9 %all-to-all-start.7 = ((bf16[2,2,88,352]{3,2,1,0:T(8,128)(2,1)}), bf16[2,2,88,352]{3,2,1,0:T(8,128)(2,1)S(1)}, u32[]{:S(2)}, u32[]{:S(2)}) async-start(bf16[2,2,88,352]{3,2,1,0:T(8,128)(2,1)} %bitcast.15), calls=%async_computation.7 | async-start | bytes 540672 | tf_op jit(solution)/shard_map/all_to_all | solution.py:42
  52.4 0.7 copy.34
  53.1 1.8 %all-to-all-done.7 = bf16[2,2,88,352]{3,2,1,0:T(8,128)(2,1)S(1)} async-done(((bf16[2,2,88,352]{3,2,1,0:T(8,128)(2,1)}), bf16[2,2,88,352]{3,2,1,0:T(8,128)(2,1)S(1)}, u32[]{:S(2)}, u32[]{:S(2)}) %all-to-all-start.7) | async-done | bytes 247840 | tf_op jit(solution)/shard_map/all_to_all | solution.py:42
  54.9 4.5 %all-to-all-start.2 = ((bf16[4,1,1,88,352]{4,3,2,1,0:T(8,128)(2,1)}), bf16[4,1,1,88,352]{4,3,2,1,0:T(8,128)(2,1)S(1)}, u32[]{:S(2)}, u32[]{:S(2)}) async-start(bf16[4,1,1,88,352]{4,3,2,1,0:T(8,128)(2,1)} %bitcast.5), calls=%async_computation.2 | async-start | bytes 540672 | tf_op jit(solution)/shard_map/all_to_all | solution.py:50
  59.5 44.1 %psum.7 = f32[3,2,4,11]{3,2,1,0:T(4,128)S(1)} all-reduce(f32[3,2,4,11]{3,2,1,0:T(4,128)S(1)} %broadcast_multiply_fusion), channel_id=1, replica_groups=mesh['dp'=4,'pipe'=2,'tensor'=4] {'dp','pipe','tensor'}, use_global_device_ids=true, to_apply=%region_3.4 | all-reduce | flops 264 | bytes 2112 | tf_op jit(solution)/shard_map/psum | solution.py:77
  103.6 0.6 dynamic-slice_multiply_fusion
  104.2 0.7 copy.38
  104.9 0.7 copy.42
  105.6 3.5 %all-to-all-start.5 = ((bf16[4,1,1,88,352]{4,3,2,1,0:T(8,128)(2,1)}), bf16[4,1,1,88,352]{4,3,2,1,0:T(8,128)(2,1)S(1)}, u32[]{:S(2)}, u32[]{:S(2)}) async-start(bf16[4,1,1,88,352]{4,3,2,1,0:T(8,128)(2,1)} %bitcast.12), calls=%async_computation.5 | async-start | bytes 540672 | tf_op jit(solution)/shard_map/all_to_all | solution.py:50
  109.3 11.6 %all_gather.9 = bf16[352,1408]{0,1:T(8,128)(2,1)S(1)} all-gather(bf16[352,352]{0,1:T(8,128)(2,1)S(1)} %copy.36), channel_id=1, replica_groups=mesh['dp'=4,'pipe'=2,'tensor'=4] {'dp'}, dimensions={1}, use_global_device_ids=true | all-gather | bytes 1239040 | tf_op jit(solution)/shard_map/all_gather | solution.py:56
  120.9 1.9 %copy.45 = bf16[352,1408]{1,0:T(8,128)(2,1)} copy(bf16[352,1408]{0,1:T(8,128)(2,1)S(1)} %all_gather.9) | data formatting | bytes 1982464
  122.8 4.8 %all-to-all-start.8 = ((bf16[4,1,1,88,352]{4,3,2,1,0:T(8,128)(2,1)}), bf16[4,1,1,88,352]{4,3,2,1,0:T(8,128)(2,1)S(1)}, u32[]{:S(2)}, u32[]{:S(2)}) async-start(bf16[4,1,1,88,352]{4,3,2,1,0:T(8,128)(2,1)} %bitcast.19), calls=%async_computation.8 | async-start | bytes 540672 | tf_op jit(solution)/shard_map/all_to_all | solution.py:50
  127.8 10.3 %all_gather.10 = bf16[352,1408]{0,1:T(8,128)(2,1)S(1)} all-gather(bf16[352,352]{0,1:T(8,128)(2,1)S(1)} %copy.40), channel_id=1, replica_groups=mesh['dp'=4,'pipe'=2,'tensor'=4] {'dp'}, dimensions={1}, use_global_device_ids=true | all-gather | bytes 1239040 | tf_op jit(solution)/shard_map/all_gather | solution.py:56
  138.1 1.9 %copy.46 = bf16[352,1408]{1,0:T(8,128)(2,1)} copy(bf16[352,1408]{0,1:T(8,128)(2,1)S(1)} %all_gather.10) | data formatting | bytes 1982464
  140.2 10.3 %all_gather.11 = bf16[352,1408]{0,1:T(8,128)(2,1)S(1)} all-gather(bf16[352,352]{0,1:T(8,128)(2,1)S(1)} %copy.44), channel_id=1, replica_groups=mesh['dp'=4,'pipe'=2,'tensor'=4] {'dp'}, dimensions={1}, use_global_device_ids=true | all-gather | bytes 1239040 | tf_op jit(solution)/shard_map/all_gather | solution.py:56
  150.5 1.9 %copy.47 = bf16[352,1408]{1,0:T(8,128)(2,1)} copy(bf16[352,1408]{0,1:T(8,128)(2,1)S(1)} %all_gather.11) | data formatting | bytes 1982464
  (25 shorter events, 1.8 us)
Async XLA Ops:
  0.6 27.4 %copy-start = (f32[1408]{0:T(1024)S(1)}, f32[1408]{0:T(1024)}, u32[]{:S(2)}) copy-start(f32[1408]{0:T(1024)} %param.8) | copy-start | bytes 16900
  0.6 6.9 %copy-start.3 = (bf16[88,1408]{1,0:T(8,128)(2,1)S(1)}, bf16[88,1408]{1,0:T(8,128)(2,1)}, u32[]{:S(2)}) copy-start(bf16[88,1408]{1,0:T(8,128)(2,1)} %param.6) | copy-start | bytes 743428
  2.7 15.1 %copy-start.2 = (bf16[88,1408]{1,0:T(8,128)(2,1)S(1)}, bf16[88,1408]{1,0:T(8,128)(2,1)}, u32[]{:S(2)}) copy-start(bf16[88,1408]{1,0:T(8,128)(2,1)} %param.7) | copy-start | bytes 743428
  2.7 10.1 %all-to-all-start = ((bf16[88,4,352]{2,0,1:T(8,128)(2,1)}), bf16[88,4,352]{2,0,1:T(8,128)(2,1)}, u32[]{:S(2)}, u32[]{:S(2)}) async-start(bf16[88,4,352]{2,0,1:T(8,128)(2,1)} %copy.33), calls=%async_computation | async-start | bytes 540672 | tf_op jit(solution)/shard_map/all_to_all | solution.py:33
  8.5 19.5 %copy-start.1 = (bf16[88,1408]{1,0:T(8,128)(2,1)S(1)}, bf16[88,1408]{1,0:T(8,128)(2,1)}, u32[]{:S(2)}) copy-start(bf16[88,1408]{1,0:T(8,128)(2,1)} %param.5) | copy-start | bytes 743428
  12.8 10.2 %all-to-all-start.3 = ((bf16[88,4,352]{2,0,1:T(8,128)(2,1)}), bf16[88,4,352]{2,0,1:T(8,128)(2,1)}, u32[]{:S(2)}, u32[]{:S(2)}) async-start(bf16[88,4,352]{2,0,1:T(8,128)(2,1)} %copy.37), calls=%async_computation.3 | async-start | bytes 540672 | tf_op jit(solution)/shard_map/all_to_all | solution.py:34
  18.0 19.0 %copy-start.4 = (f32[1408]{0:T(1024)S(1)}, f32[1408]{0:T(1024)}, u32[]{:S(2)}) copy-start(f32[1408]{0:T(1024)} %param.9) | copy-start | bytes 16900
  23.0 10.2 %all-to-all-start.6 = ((bf16[88,4,352]{2,0,1:T(8,128)(2,1)}), bf16[88,4,352]{2,0,1:T(8,128)(2,1)}, u32[]{:S(2)}, u32[]{:S(2)}) async-start(bf16[88,4,352]{2,0,1:T(8,128)(2,1)} %copy.41), calls=%async_computation.6 | async-start | bytes 540672 | tf_op jit(solution)/shard_map/all_to_all | solution.py:35
  33.2 6.0 %all-to-all-start.1 = ((bf16[2,2,88,352]{3,2,1,0:T(8,128)(2,1)}), bf16[2,2,88,352]{3,2,1,0:T(8,128)(2,1)S(1)}, u32[]{:S(2)}, u32[]{:S(2)}) async-start(bf16[2,2,88,352]{3,2,1,0:T(8,128)(2,1)} %bitcast.1), calls=%async_computation.1 | async-start | bytes 540672 | tf_op jit(solution)/shard_map/all_to_all | solution.py:42
  39.2 8.1 %all-to-all-start.4 = ((bf16[2,2,88,352]{3,2,1,0:T(8,128)(2,1)}), bf16[2,2,88,352]{3,2,1,0:T(8,128)(2,1)S(1)}, u32[]{:S(2)}, u32[]{:S(2)}) async-start(bf16[2,2,88,352]{3,2,1,0:T(8,128)(2,1)} %bitcast.8), calls=%async_computation.4 | async-start | bytes 540672 | tf_op jit(solution)/shard_map/all_to_all | solution.py:42
  47.4 7.5 %all-to-all-start.7 = ((bf16[2,2,88,352]{3,2,1,0:T(8,128)(2,1)}), bf16[2,2,88,352]{3,2,1,0:T(8,128)(2,1)S(1)}, u32[]{:S(2)}, u32[]{:S(2)}) async-start(bf16[2,2,88,352]{3,2,1,0:T(8,128)(2,1)} %bitcast.15), calls=%async_computation.7 | async-start | bytes 540672 | tf_op jit(solution)/shard_map/all_to_all | solution.py:42
  54.9 50.7 %all-to-all-start.2 = ((bf16[4,1,1,88,352]{4,3,2,1,0:T(8,128)(2,1)}), bf16[4,1,1,88,352]{4,3,2,1,0:T(8,128)(2,1)S(1)}, u32[]{:S(2)}, u32[]{:S(2)}) async-start(bf16[4,1,1,88,352]{4,3,2,1,0:T(8,128)(2,1)} %bitcast.5), calls=%async_computation.2 | async-start | bytes 540672 | tf_op jit(solution)/shard_map/all_to_all | solution.py:50
  105.6 17.2 %all-to-all-start.5 = ((bf16[4,1,1,88,352]{4,3,2,1,0:T(8,128)(2,1)}), bf16[4,1,1,88,352]{4,3,2,1,0:T(8,128)(2,1)S(1)}, u32[]{:S(2)}, u32[]{:S(2)}) async-start(bf16[4,1,1,88,352]{4,3,2,1,0:T(8,128)(2,1)} %bitcast.12), calls=%async_computation.5 | async-start | bytes 540672 | tf_op jit(solution)/shard_map/all_to_all | solution.py:50
  122.8 17.2 %all-to-all-start.8 = ((bf16[4,1,1,88,352]{4,3,2,1,0:T(8,128)(2,1)}), bf16[4,1,1,88,352]{4,3,2,1,0:T(8,128)(2,1)S(1)}, u32[]{:S(2)}, u32[]{:S(2)}) async-start(bf16[4,1,1,88,352]{4,3,2,1,0:T(8,128)(2,1)} %bitcast.19), calls=%async_computation.8 | async-start | bytes 540672 | tf_op jit(solution)/shard_map/all_to_all | solution.py:50
where the time goes:
time: 155 us; the launch traced here: 152 us
  blocking collectives  76.3 us (49%)
  starting transfers between devices  41.5 us (27%)
  waiting for transfers between devices  19.5 us (13%)
  local copies, waits for them, and re-layouts  12.5 us (8%)
    psum x1, blocking collectives, shards(): summed = lax.psum(spread, ('dp', 'pipe', 'tensor'))  44.1 us
    all_gather x3, blocking collectives, shards(): lax.all_gather(for_sending(flat_pieces), 'dp', axis=1, tiled=True)  32.2 us
    all_to_all x3, starting transfers between devices, shards(): lax.all_to_all(for_sending(grouped), 'pipe', split_axis=0, concat_axis=2,...  13.9 us
    all_to_all x3, starting transfers between devices, shards(): lax.all_to_all(for_sending(routed), 'tensor', split_axis=0, concat_axis=2...  12.8 us
    all_to_all x3, waiting for transfers between devices, shards(): lax.all_to_all(for_sending(grouped), 'pipe', split_axis=0, concat_axis=2,...  6.49 us
    unnamed x13, local copies, waits for them, and re-layouts  5.65 us
    all_to_all x1, starting transfers between devices, shards(): lax.all_to_all(sources[2], 'dp', split_axis=1, concat_axis=0, tiled=True)  5.01 us
    all_to_all x1, starting transfers between devices, shards(): lax.all_to_all(sources[1], 'dp', split_axis=1, concat_axis=0, tiled=True)  5 us
  transfers between devices with their start and end apart: 9, of which 6 were waited for; matrix products, arithmetic and copies ran while one was open for 6% of the time, Pallas kernels for 0%

commit v1 on v0

--- a/solution.py
+++ b/solution.py
@@ -1,6 +1,10 @@
+import functools
+
 import jax
 import jax.numpy as jnp
 from jax import lax
+from jax.experimental import pallas as pl
+from jax.experimental.pallas import tpu as pltpu
 from jax.sharding import PartitionSpec as P
 
 CHECK_COLS = 128
@@ -82,9 +86,285 @@
     return (tiles[0], tiles[1], tiles[2], checks)
 
 
+def remote(src, dst, send_sem, recv_sem, where):
+    return pltpu.make_async_remote_copy(
+        src_ref=src,
+        dst_ref=dst,
+        send_sem=send_sem,
+        recv_sem=recv_sem,
+        device_id=where,
+        device_id_type=pl.DeviceIdType.MESH,
+    )
+
+
+def route(
+    count,
+    w_ref,
+    m_ref,
+    v_ref,
+    row_ref,
+    col_ref,
+    out0,
+    out1,
+    out2,
+    check_ref,
+    src,
+    crossed,
+    own,
+    transit,
+    acc,
+    row_terms,
+    load_sem,
+    cross_send,
+    cross_recv,
+    z_send,
+    own_recv,
+    transit_recv,
+    x_send,
+    y_send,
+    d_send,
+    out_sem,
+):
+    dp, y, z = lax.axis_index("dp"), lax.axis_index("pipe"), lax.axis_index("tensor")
+    x, core = dp // 2, dp % 2
+    active = z // 2 == core
+    diag = x == y
+    to_x = {"dp": (1 - x) * 2 + core, "pipe": y, "tensor": z}
+    to_y = {"dp": dp, "pipe": 1 - y, "tensor": z}
+    to_core = {"dp": x * 2 + 1 - core, "pipe": y, "tensor": z}
+
+    def to_z(pos):
+        return {"dp": dp, "pipe": y, "tensor": pos}
+
+    rows, width = w_ref.shape
+    ins = (w_ref, m_ref, v_ref)
+    outs = (out0, out1, out2)
+    loads = [pltpu.make_async_copy(ins[a], src.at[a], load_sem.at[a]) for a in range(3)]
+    for load in loads:
+        load.start()
+
+    barrier = pltpu.get_barrier_semaphore()
+    for where in (to_x, to_y, to_core):
+        pl.semaphore_signal(barrier, inc=1, device_id=where, device_id_type=pl.DeviceIdType.MESH)
+    for step in range(1, count):
+        pl.semaphore_signal(
+            barrier,
+            inc=1,
+            device_id=to_z((z + step) % count),
+            device_id_type=pl.DeviceIdType.MESH,
+        )
+    pl.semaphore_wait(barrier, count + 2)
+    for load in loads:
+        load.wait()
+
+    cross_a = remote(src.at[2], crossed.at[0], cross_send.at[0], cross_recv.at[0], to_y)
+    cross_b = [
+        remote(src.at[a], crossed.at[a], cross_send.at[a], cross_recv.at[a], to_y) for a in range(2)
+    ]
+
+    def z_copies(pos, turn, pieces, act):
+        for a, piece, slot, sem in pieces:
+            away = remote(piece, slot, z_send.at[turn, a], sem, to_z(pos))
+            near = pltpu.make_async_copy(piece, slot, sem)
+
+            @pl.when(pos != z)
+            def _():
+                if act == "start":
+                    away.start()
+                else:
+                    away.wait_send()
+
+            if act == "start":
+
+                @pl.when(pos == z)
+                def _():
+                    near.start()
+
+    mine, other = 2 * core + y, 2 * core + 1 - y
+    diag_mine = [(a, src.at[a], own.at[a, z], own_recv.at[a, z]) for a in range(2)]
+    diag_other = [(a, crossed.at[a], own.at[a, z], own_recv.at[a, z]) for a in range(2)]
+    off_mine = [(0, src.at[2], transit.at[z], transit_recv.at[z])]
+    off_other = [(0, crossed.at[0], transit.at[z], transit_recv.at[z])]
+
+    @pl.when(diag)
+    def _():
+        cross_a.start()
+        z_copies(mine, 0, diag_mine, "start")
+
+    @pl.when(jnp.logical_not(diag))
+    def _():
+        for copy in cross_b:
+            copy.start()
+        z_copies(mine, 0, off_mine, "start")
+
+    for k in range(count):
+        first = (z * count + k) * rows
+        everyone = jnp.broadcast_to(row_ref[...].reshape(1, width), (8, width))
+        part = pltpu.roll(everyone, (width - first) % width, 1)[:, :rows]
+        high = part.astype(jnp.bfloat16).astype(jnp.float32)
+        middle = (part - high).astype(jnp.bfloat16).astype(jnp.float32)
+        low = part - high - middle
+        line = lax.broadcasted_iota(jnp.int32, (8, rows), 0)
+        terms = jnp.where(
+            line == 0, high, jnp.where(line == 1, middle, jnp.where(line == 2, low, 0.0))
+        )
+        row_terms[k] = terms.astype(jnp.bfloat16)
+    acc[...] = jnp.zeros_like(acc)
+
+    @pl.when(diag)
+    def _():
+        for copy in cross_b:
+            copy.wait_recv()
+        z_copies(other, 1, diag_other, "start")
+
+    @pl.when(jnp.logical_not(diag))
+    def _():
+        cross_a.wait_recv()
+        z_copies(other, 1, off_other, "start")
+
+    def arrived(a, k):
+        pltpu.make_async_copy(own.at[a, k], own.at[a, k], own_recv.at[a, k]).wait()
+
+    def passed(k):
+        pltpu.make_async_copy(transit.at[k], transit.at[k], transit_recv.at[k]).wait()
+
+    def own_x(a, k):
+        return remote(own.at[a, k], own.at[a, k], x_send.at[a, k], own_recv.at[a, k], to_x)
+
+    def transit_x(k):
+        return remote(transit.at[k], transit.at[k], x_send.at[0, k], transit_recv.at[k], to_x)
+
+    def transit_y(k):
+        return remote(transit.at[k], own.at[2, k], y_send.at[k], own_recv.at[2, k], to_y)
+
+    def across(a, k):
+        return remote(own.at[a, k], own.at[a, k], d_send.at[a, k], own_recv.at[a, k], to_core)
+
+    def leave(a, k):
+        return pltpu.make_async_copy(own.at[a, k], outs[a].at[k], out_sem.at[a, k])
+
+    @pl.loop(0, count)
+    def _(step):
+        k = jnp.where(z < count // 2, (z + step) % count, (z + count - step) % count)
+
+        @pl.when(jnp.logical_and(active, diag))
+        def _():
+            for a in range(2):
+                arrived(a, k)
+                own_x(a, k).start()
+                across(a, k).start()
+            passed(k)
+            transit_y(k).start()
+            arrived(2, k)
+            across(2, k).start()
+
+        @pl.when(jnp.logical_and(active, jnp.logical_not(diag)))
+        def _():
+            passed(k)
+            transit_y(k).start()
+            transit_x(k).start()
+            for a in range(3):
+                arrived(a, k)
+                across(a, k).start()
+
+        @pl.when(jnp.logical_not(active))
+        def _():
+            for a in range(3):
+                arrived(a, k)
+
+        for a in range(3):
+            leave(a, k).start()
+
+        for a in range(3):
+            acc[a] += jnp.dot(row_terms[k], own[a, k], preferred_element_type=jnp.float32)
+
+    factor = float(rows * count * CHECK_COLS) ** (-0.5)
+    blocks = width // CHECK_COLS
+    weight = col_ref[...].reshape(1, width)
+    for a in range(3):
+        mixed = jnp.sum(acc[a], axis=0, keepdims=True) * weight
+        lane = lax.broadcasted_iota(jnp.int32, (1, blocks), 1)
+        line = jnp.zeros((1, blocks), jnp.float32)
+        for e in range(blocks):
+            part = jnp.sum(mixed[:, e * CHECK_COLS : (e + 1) * CHECK_COLS], axis=1, keepdims=True)
+            line = jnp.where(lane == e, part, line)
+        check_ref[a, 0] = line * factor
+
+    @pl.when(diag)
+    def _():
+        cross_a.wait_send()
+        z_copies(mine, 0, diag_mine, "wait")
+        z_copies(other, 1, diag_other, "wait")
+
+    @pl.when(jnp.logical_not(diag))
+    def _():
+        for copy in cross_b:
+            copy.wait_send()
+        z_copies(mine, 0, off_mine, "wait")
+        z_copies(other, 1, off_other, "wait")
+
+    @pl.loop(0, count)
+    def _(k):
+        @pl.when(active)
+        def _():
+            for a in range(3):
+                across(a, k).wait_send()
+            transit_y(k).wait_send()
+
+            @pl.when(diag)
+            def _():
+                for a in range(2):
+                    own_x(a, k).wait_send()
+
+            @pl.when(jnp.logical_not(diag))
+            def _():
+                transit_x(k).wait_send()
+
+        for a in range(3):
+            leave(a, k).wait()
+
+
+def routed(weights, first_moment, second_moment, row_weight, col_weight):
+    count = lax.axis_size("dp")
+    rows, width = weights.shape
+    blocks = width // CHECK_COLS
+    vmem = pl.BlockSpec(memory_space=pltpu.VMEM)
+    anywhere = pl.BlockSpec(memory_space=pl.ANY)
+    tile = jax.ShapeDtypeStruct((count, rows, width), weights.dtype)
+    dma = pltpu.SemaphoreType.DMA
+    out = pl.pallas_call(
+        functools.partial(route, count),
+        out_shape=(tile, tile, tile, jax.ShapeDtypeStruct((3, 1, 1, blocks), jnp.float32)),
+        in_specs=[anywhere, anywhere, anywhere, vmem, vmem],
+        out_specs=(anywhere, anywhere, anywhere, vmem),
+        scratch_shapes=[
+            pltpu.VMEM((3, rows, width), weights.dtype),
+            pltpu.VMEM((2, rows, width), weights.dtype),
+            pltpu.VMEM((3, count, rows, width), weights.dtype),
+            pltpu.VMEM((count, rows, width), weights.dtype),
+            pltpu.VMEM((3, 8, width), jnp.float32),
+            pltpu.VMEM((count, 8, rows), jnp.bfloat16),
+            dma((3,)),
+            dma((2,)),
+            dma((2,)),
+            dma((2, 2)),
+            dma((3, count)),
+            dma((count,)),
+            dma((2, count)),
+            dma((count,)),
+            dma((3, count)),
+            dma((3, count)),
+        ],
+        compiler_params=pltpu.CompilerParams(collective_id=0, has_side_effects=True),
+    )(weights, first_moment, second_moment, row_weight, col_weight)
+    return tuple(item.reshape(count * rows, width) for item in out[:3]) + (out[3],)
+
+
 def solution(mesh):
+    dp_count, pipe_count, tensor_count = (mesh.shape[a] for a in ("dp", "pipe", "tensor"))
+    square = dp_count == tensor_count == 2 * pipe_count and pipe_count == 2
     return jax.shard_map(
-        shards,
+        routed if square else shards,
         mesh=mesh,
         in_specs=(
             P(("dp", "pipe", "tensor"), None),

time: 155 us -> 71 us (0.46); the launches traced: 152 us -> 70.7 us
  blocking collectives: 76.3 us -> 0 us
  Pallas kernels: 0 us -> 64.7 us
  starting transfers between devices: 41.5 us -> 0 us
  waiting for transfers between devices: 19.5 us -> 0 us
  local copies, waits for them, and re-layouts: 12.5 us -> 5.39 us
    pallas_call x0 -> x1, Pallas kernels: none -> 64.7 us  [routed(): pl.pallas_call(functools.partial(route, count), out_shape=(tile, tile, ti...]
    psum x1 -> x0, blocking collectives: 44.1 us -> none  [shards(): summed = lax.psum(spread, ('dp', 'pipe', 'tensor'))]
    all_to_all x9 -> x0, starting transfers between devices: 41.5 us -> none  [the longest x3 13.9 us: shards(): lax.all_to_all(for_sending(grouped), 'pipe', split_axis=0, concat_axis=2,...]
    all_gather x3 -> x0, blocking collectives: 32.2 us -> none  [shards(): lax.all_gather(for_sending(flat_pieces), 'dp', axis=1, tiled=True)]
    all_to_all x9 -> x0, waiting for transfers between devices: 19.5 us -> none  [the longest x3 6.49 us: shards(): lax.all_to_all(for_sending(grouped), 'pipe', split_axis=0, concat_axis=2,...]
    all_to_all x9 -> x0, local copies, waits for them, and re-layouts: 6.22 us -> none  [the longest x3 2.18 us: shards(): lax.all_to_all(for_sending(grouped), 'pipe', split_axis=0, concat_axis=2,...]
    unnamed x13 -> x10, local copies, waits for them, and re-layouts: 5.65 us -> 5.39 us
  transfers between devices with their start and end apart: 9 -> 0, of which waited for: 6 -> 0; matrix products, arithmetic and copies ran while one was open for 6% -> 0% of each run, Pallas kernels for 0% -> 0%
where the time goes in v1:
time: 71 us; the launch traced here: 70.7 us
  Pallas kernels  64.7 us (91%)
  local copies, waits for them, and re-layouts  5.39 us (8%)
    pallas_call x1, Pallas kernels, routed(): pl.pallas_call(functools.partial(route, count), out_shape=(tile, tile, ti...  64.7 us
    unnamed x10, local copies, waits for them, and re-layouts  5.39 us

profile of v1, /device:TPU:5, one launch (start us, length us, event | category | flops | bytes accessed | tf_op | source)
XLA Modules:
  0.0 70.7 jit_solution(14869273863420870840)
XLA Ops:
  0.6 64.7 %shard_map.84 = (bf16[4,88,1408]{2,1,0:T(8,128)(2,1)}, bf16[4,88,1408]{2,1,0:T(8,128)(2,1)}, bf16[4,88,1408]{2,1,0:T(8,128)(2,1)}, f32[3,1,1,11]{3,2,1,0:T(1,128)}) custom-call(bf16[88,1408]{1,0:T(8,128)(2,1)} %w_ref.1, bf16[88,1408]{1,0:T(8,128)(2,1)} %m_ref.1, bf16[88,1408]{1,0:T(8,128)(2,1)} %v_ref.1, f32[1408]{0:T(1024)} %row_ref.1, f32[1408]{0:T(1024)} %col_ref.1), custom_call_target="tpu_custom_call" | custom-call | tf_op jit(solution)/shard_map/pallas_call | solution.py:335
  65.3 0.0 copy-start.1
  65.3 2.3 %copy.13 = bf16[352,1408]{1,0:T(8,128)(2,1)} copy(bf16[352,1408]{1,0:T(8,128)(2,1)} %bitcast.5) | data formatting | bytes 1982464
  67.7 0.0 copy-done.1
  67.7 0.0 copy-start
  67.7 0.9 %copy.14 = bf16[352,1408]{1,0:T(8,128)(2,1)} copy(bf16[352,1408]{1,0:T(8,128)(2,1)S(1)} %bitcast.4) | data formatting | bytes 1982464
  68.6 0.6 copy-done
  69.2 0.0 copy-start.2
  69.2 0.9 %copy.15 = bf16[352,1408]{1,0:T(8,128)(2,1)} copy(bf16[352,1408]{1,0:T(8,128)(2,1)S(1)} %bitcast.3) | data formatting | bytes 1982464
  70.2 0.0 copy-done.2
  70.2 0.6 copy.16
Async XLA Ops:
  65.3 2.3 %copy-start.1 = (bf16[4,88,1408]{2,1,0:T(8,128)(2,1)S(1)}, bf16[4,88,1408]{2,1,0:T(8,128)(2,1)}, u32[]{:S(2)}) copy-start(bf16[4,88,1408]{2,1,0:T(8,128)(2,1)} %get-tuple-element.9) | copy-start | bytes 2973700
  67.7 1.6 %copy-start = (bf16[4,88,1408]{2,1,0:T(8,128)(2,1)S(1)}, bf16[4,88,1408]{2,1,0:T(8,128)(2,1)}, u32[]{:S(2)}) copy-start(bf16[4,88,1408]{2,1,0:T(8,128)(2,1)} %get-tuple-element.10) | copy-start | bytes 2973700
  69.2 1.0 %copy-start.2 = (f32[3,1,1,11]{3,2,1,0:T(1,128)S(1)}, f32[3,1,1,11]{3,2,1,0:T(1,128)}, u32[]{:S(2)}) copy-start(f32[3,1,1,11]{3,2,1,0:T(1,128)} %get-tuple-element.19) | copy-start | bytes 400

commit v2 on v1

--- a/solution.py
+++ b/solution.py
@@ -102,18 +102,10 @@
     w_ref,
     m_ref,
     v_ref,
-    row_ref,
-    col_ref,
-    out0,
-    out1,
-    out2,
-    check_ref,
+    own,
     src,
     crossed,
-    own,
     transit,
-    acc,
-    row_terms,
     load_sem,
     cross_send,
     cross_recv,
@@ -123,7 +115,6 @@
     x_send,
     y_send,
     d_send,
-    out_sem,
 ):
     dp, y, z = lax.axis_index("dp"), lax.axis_index("pipe"), lax.axis_index("tensor")
     x, core = dp // 2, dp % 2
@@ -136,9 +127,7 @@
     def to_z(pos):
         return {"dp": dp, "pipe": y, "tensor": pos}
 
-    rows, width = w_ref.shape
     ins = (w_ref, m_ref, v_ref)
-    outs = (out0, out1, out2)
     loads = [pltpu.make_async_copy(ins[a], src.at[a], load_sem.at[a]) for a in range(3)]
     for load in loads:
         load.start()
@@ -157,10 +146,8 @@
     for load in loads:
         load.wait()
 
-    cross_a = remote(src.at[2], crossed.at[0], cross_send.at[0], cross_recv.at[0], to_y)
-    cross_b = [
-        remote(src.at[a], crossed.at[a], cross_send.at[a], cross_recv.at[a], to_y) for a in range(2)
-    ]
+    def cross(a):
+        return remote(src.at[a], crossed, cross_send, cross_recv, to_y)
 
     def z_copies(pos, turn, pieces, act):
         for a, piece, slot, sem in pieces:
@@ -181,24 +168,134 @@
                     near.start()
 
     mine, other = 2 * core + y, 2 * core + 1 - y
-    diag_mine = [(a, src.at[a], own.at[a, z], own_recv.at[a, z]) for a in range(2)]
-    diag_other = [(a, crossed.at[a], own.at[a, z], own_recv.at[a, z]) for a in range(2)]
-    off_mine = [(0, src.at[2], transit.at[z], transit_recv.at[z])]
-    off_other = [(0, crossed.at[0], transit.at[z], transit_recv.at[z])]
+    diag_mine = [(a, src.at[a], own.at[a, z], own_recv.at[a, z]) for a in (0, 1)]
+    diag_other = [(0, crossed, own.at[0, z], own_recv.at[0, z])]
+    off_mine = [(a - 1, src.at[a], transit.at[a - 1, z], transit_recv.at[a - 1, z]) for a in (1, 2)]
+    off_other = [(0, crossed, transit.at[1, z], transit_recv.at[1, z])]
 
     @pl.when(diag)
     def _():
-        cross_a.start()
+        cross(2).start()
         z_copies(mine, 0, diag_mine, "start")
+        cross(2).wait_recv()
+        z_copies(other, 1, diag_other, "start")
 
     @pl.when(jnp.logical_not(diag))
     def _():
-        for copy in cross_b:
-            copy.start()
+        cross(0).start()
         z_copies(mine, 0, off_mine, "start")
-
+        cross(0).wait_recv()
+        z_copies(other, 1, off_other, "start")
+
+    def arrived(a, k):
+        pltpu.make_async_copy(own.at[a, k], own.at[a, k], own_recv.at[a, k]).wait()
+
+    def passed(a, k):
+        slot = transit.at[a - 1, k]
+        pltpu.make_async_copy(slot, slot, transit_recv.at[a - 1, k]).wait()
+
+    def own_x(a, k):
+        return remote(own.at[a, k], own.at[a, k], x_send.at[a, k], own_recv.at[a, k], to_x)
+
+    def transit_x(a, k):
+        slot = transit.at[a - 1, k]
+        return remote(slot, slot, x_send.at[a - 1, k], transit_recv.at[a - 1, k], to_x)
+
+    def transit_y(a, k):
+        return remote(
+            transit.at[a - 1, k], own.at[a, k], y_send.at[a - 1, k], own_recv.at[a, k], to_y
+        )
+
+    def across(a, k):
+        return remote(own.at[a, k], own.at[a, k], d_send.at[a, k], own_recv.at[a, k], to_core)
+
+    half = count // 2
+
+    def piece(step):
+        if step < half:
+            return jnp.where(
+                z < half, (z + half - step) % half, half + (z - half + half - step) % half
+            )
+        return jnp.where(z < half, step, count - 1 - step)
+
+    match = z % 2 == y
+
+    def forward(on_diag, on_match):
+        direct, passing, late = ((0, 1), (1, 2), (2,)) if on_match else ((0,), (2,), (1, 2))
+        for step in range(count + 2):
+            if step < count:
+                k = piece(step)
+                if on_diag:
+                    for a in direct:
+                        arrived(a, k)
+                        own_x(a, k).start()
+                        across(a, k).start()
+                else:
+                    for a in passing:
+                        passed(a, k)
+                        transit_x(a, k).start()
+                        transit_y(a, k).start()
+            if 1 <= step <= count:
+                k = piece(step - 1)
+                if on_diag:
+                    for a in passing:
+                        passed(a, k)
+                        transit_y(a, k).start()
+                else:
+                    for a in direct:
+                        arrived(a, k)
+                        across(a, k).start()
+            if step >= 2:
+                k = piece(step - 2)
+                for a in late:
+                    arrived(a, k)
+                    across(a, k).start()
+        for k in range(count):
+            for a in range(3):
+                across(a, k).wait_send()
+            for a in passing:
+                transit_y(a, k).wait_send()
+                if not on_diag:
+                    transit_x(a, k).wait_send()
+            if on_diag:
+                for a in direct:
+                    own_x(a, k).wait_send()
+
+    for on_diag in (True, False):
+        for on_match in (True, False):
+
+            @pl.when(active & (diag == on_diag) & (match == on_match))
+            def _():
+                forward(on_diag, on_match)
+
+    @pl.when(jnp.logical_not(active))
+    def _():
+        for k in range(count):
+            for a in range(3):
+                arrived(a, k)
+
+    @pl.when(diag)
+    def _():
+        cross(2).wait_send()
+        z_copies(mine, 0, diag_mine, "wait")
+        z_copies(other, 1, diag_other, "wait")
+
+    @pl.when(jnp.logical_not(diag))
+    def _():
+        cross(0).wait_send()
+        z_copies(mine, 0, off_mine, "wait")
+        z_copies(other, 1, off_other, "wait")
+
+
+def finish(count, own, row_ref, col_ref, out0, out1, out2, check_ref, acc, out_sem):
+    rows, width = own.shape[2:]
+    outs = (out0, out1, out2)
+    leaving = [pltpu.make_async_copy(own.at[a], outs[a], out_sem.at[a]) for a in range(3)]
+    for copy in leaving:
+        copy.start()
+    acc[...] = jnp.zeros_like(acc)
     for k in range(count):
-        first = (z * count + k) * rows
+        first = (lax.axis_index("tensor") * count + k) * rows
         everyone = jnp.broadcast_to(row_ref[...].reshape(1, width), (8, width))
         part = pltpu.roll(everyone, (width - first) % width, 1)[:, :rows]
         high = part.astype(jnp.bfloat16).astype(jnp.float32)
@@ -208,75 +305,9 @@
         terms = jnp.where(
             line == 0, high, jnp.where(line == 1, middle, jnp.where(line == 2, low, 0.0))
         )
-        row_terms[k] = terms.astype(jnp.bfloat16)
-    acc[...] = jnp.zeros_like(acc)
-
-    @pl.when(diag)
-    def _():
-        for copy in cross_b:
-            copy.wait_recv()
-        z_copies(other, 1, diag_other, "start")
-
-    @pl.when(jnp.logical_not(diag))
-    def _():
-        cross_a.wait_recv()
-        z_copies(other, 1, off_other, "start")
-
-    def arrived(a, k):
-        pltpu.make_async_copy(own.at[a, k], own.at[a, k], own_recv.at[a, k]).wait()
-
-    def passed(k):
-        pltpu.make_async_copy(transit.at[k], transit.at[k], transit_recv.at[k]).wait()
-
-    def own_x(a, k):
-        return remote(own.at[a, k], own.at[a, k], x_send.at[a, k], own_recv.at[a, k], to_x)
-
-    def transit_x(k):
-        return remote(transit.at[k], transit.at[k], x_send.at[0, k], transit_recv.at[k], to_x)
-
-    def transit_y(k):
-        return remote(transit.at[k], own.at[2, k], y_send.at[k], own_recv.at[2, k], to_y)
-
-    def across(a, k):
-        return remote(own.at[a, k], own.at[a, k], d_send.at[a, k], own_recv.at[a, k], to_core)
-
-    def leave(a, k):
-        return pltpu.make_async_copy(own.at[a, k], outs[a].at[k], out_sem.at[a, k])
-
-    @pl.loop(0, count)
-    def _(step):
-        k = jnp.where(z < count // 2, (z + step) % count, (z + count - step) % count)
-
-        @pl.when(jnp.logical_and(active, diag))
-        def _():
-            for a in range(2):
-                arrived(a, k)
-                own_x(a, k).start()
-                across(a, k).start()
-            passed(k)
-            transit_y(k).start()
-            arrived(2, k)
-            across(2, k).start()
-
-        @pl.when(jnp.logical_and(active, jnp.logical_not(diag)))
-        def _():
-            passed(k)
-            transit_y(k).start()
-            transit_x(k).start()
-            for a in range(3):
-                arrived(a, k)
-                across(a, k).start()
-
-        @pl.when(jnp.logical_not(active))
-        def _():
-            for a in range(3):
-                arrived(a, k)
-
+        terms = terms.astype(jnp.bfloat16)
         for a in range(3):
-            leave(a, k).start()
-
-        for a in range(3):
-            acc[a] += jnp.dot(row_terms[k], own[a, k], preferred_element_type=jnp.float32)
+            acc[a] += jnp.dot(terms, own[a, k], preferred_element_type=jnp.float32)
 
     factor = float(rows * count * CHECK_COLS) ** (-0.5)
     blocks = width // CHECK_COLS
@@ -289,39 +320,8 @@
             part = jnp.sum(mixed[:, e * CHECK_COLS : (e + 1) * CHECK_COLS], axis=1, keepdims=True)
             line = jnp.where(lane == e, part, line)
         check_ref[a, 0] = line * factor
-
-    @pl.when(diag)
-    def _():
-        cross_a.wait_send()
-        z_copies(mine, 0, diag_mine, "wait")
-        z_copies(other, 1, diag_other, "wait")
-
-    @pl.when(jnp.logical_not(diag))
-    def _():
-        for copy in cross_b:
-            copy.wait_send()
-        z_copies(mine, 0, off_mine, "wait")
-        z_copies(other, 1, off_other, "wait")
-
-    @pl.loop(0, count)
-    def _(k):
-        @pl.when(active)
-        def _():
-            for a in range(3):
-                across(a, k).wait_send()
-            transit_y(k).wait_send()
-
-            @pl.when(diag)
-            def _():
-                for a in range(2):
-                    own_x(a, k).wait_send()
-
-            @pl.when(jnp.logical_not(diag))
-            def _():
-                transit_x(k).wait_send()
-
-        for a in range(3):
-            leave(a, k).wait()
+    for copy in leaving:
+        copy.wait()
 
 
 def routed(weights, first_moment, second_moment, row_weight, col_weight):
@@ -332,31 +332,37 @@
     anywhere = pl.BlockSpec(memory_space=pl.ANY)
     tile = jax.ShapeDtypeStruct((count, rows, width), weights.dtype)
     dma = pltpu.SemaphoreType.DMA
-    out = pl.pallas_call(
+    own = pl.pallas_call(
         functools.partial(route, count),
-        out_shape=(tile, tile, tile, jax.ShapeDtypeStruct((3, 1, 1, blocks), jnp.float32)),
-        in_specs=[anywhere, anywhere, anywhere, vmem, vmem],
-        out_specs=(anywhere, anywhere, anywhere, vmem),
+        out_shape=pltpu.VMEM((3, count, rows, width), weights.dtype),
+        in_specs=[anywhere] * 3,
+        out_specs=vmem,
         scratch_shapes=[
             pltpu.VMEM((3, rows, width), weights.dtype),
-            pltpu.VMEM((2, rows, width), weights.dtype),
-            pltpu.VMEM((3, count, rows, width), weights.dtype),
-            pltpu.VMEM((count, rows, width), weights.dtype),
-            pltpu.VMEM((3, 8, width), jnp.float32),
-            pltpu.VMEM((count, 8, rows), jnp.bfloat16),
+            pltpu.VMEM((rows, width), weights.dtype),
+            pltpu.VMEM((2, count, rows, width), weights.dtype),
             dma((3,)),
-            dma((2,)),
-            dma((2,)),
+            dma(()),
+            dma(()),
             dma((2, 2)),
             dma((3, count)),
-            dma((count,)),
             dma((2, count)),
-            dma((count,)),
-            dma((3, count)),
+            dma((2, count)),
+            dma((2, count)),
             dma((3, count)),
         ],
-        compiler_params=pltpu.CompilerParams(collective_id=0, has_side_effects=True),
-    )(weights, first_moment, second_moment, row_weight, col_weight)
+        compiler_params=pltpu.CompilerParams(
+            collective_id=0, has_side_effects=True
+        ),
+    )(weights, first_moment, second_moment)
+    out = pl.pallas_call(
+        functools.partial(finish, count),
+        out_shape=(tile, tile, tile, jax.ShapeDtypeStruct((3, 1, 1, blocks), jnp.float32)),
+        in_specs=[vmem, vmem, vmem],
+        out_specs=(anywhere, anywhere, anywhere, vmem),
+        scratch_shapes=[pltpu.VMEM((3, 8, width), jnp.float32), dma((3,))],
+        compiler_params=pltpu.CompilerParams(vmem_limit_bytes=16 * 1024 * 1024),
+    )(own, row_weight, col_weight)
     return tuple(item.reshape(count * rows, width) for item in out[:3]) + (out[3],)
 
 

time: 71 us -> 50.4 us (0.71)
  Pallas kernels: 64.7 us -> 49.6 us
  local copies, waits for them, and re-layouts: 5.39 us -> 0.01 us
    pallas_call x1 -> x2, Pallas kernels: 64.7 us -> 49.6 us  [the longest x1 47.2 us: routed(): pl.pallas_call(functools.partial(route, count), out_shape=pltpu.VMEM((3,...]
    unnamed x10 -> x4, local copies, waits for them, and re-layouts: 5.39 us -> 0.01 us
where the time goes in v2:
time: 50.4 us; the launch traced here: 50.3 us
  Pallas kernels  49.6 us (98%)
  between operations  0.67 us (1%)
    pallas_call x1, Pallas kernels, routed(): pl.pallas_call(functools.partial(route, count), out_shape=pltpu.VMEM((3,...  47.2 us
    pallas_call x1, Pallas kernels, routed(): pl.pallas_call(functools.partial(finish, count), out_shape=(tile, tile, t...  2.38 us

profile of v2, /device:TPU:5, one launch (start us, length us, event | category | flops | bytes accessed | tf_op | source)
XLA Modules:
  0.0 50.3 jit_solution(4514547940744367606)
XLA Ops:
  0.6 0.0 copy-start.1
  0.6 0.0 copy-start
  0.7 47.2 %shard_map.84.own = bf16[3,4,88,1408]{3,2,1,0:T(8,128)(2,1)S(1)} custom-call(bf16[88,1408]{1,0:T(8,128)(2,1)} %w_ref.1, bf16[88,1408]{1,0:T(8,128)(2,1)} %m_ref.1, bf16[88,1408]{1,0:T(8,128)(2,1)} %v_ref.1), custom_call_target="tpu_custom_call" | custom-call | tf_op jit(solution)/shard_map/pallas_call | solution.py:335
  47.9 0.0 copy-done.1
  47.9 0.0 copy-done
  47.9 2.4 %shard_map.85 = (bf16[4,88,1408]{2,1,0:T(8,128)(2,1)}, bf16[4,88,1408]{2,1,0:T(8,128)(2,1)}, bf16[4,88,1408]{2,1,0:T(8,128)(2,1)}, f32[3,1,1,11]{3,2,1,0:T(1,128)}) custom-call(bf16[3,4,88,1408]{3,2,1,0:T(8,128)(2,1)S(1)} %shard_map.84.own, f32[1408]{0:T(1024)S(1)} %copy-done, f32[1408]{0:T(1024)S(1)} %copy-done.1), custom_call_target="tpu_custom_call" | custom-call | tf_op jit(solution)/shard_map/pallas_call | solution.py:358
Async XLA Ops:
  0.6 47.2 %copy-start.1 = (f32[1408]{0:T(1024)S(1)}, f32[1408]{0:T(1024)}, u32[]{:S(2)}) copy-start(f32[1408]{0:T(1024)} %col_ref.1) | copy-start | bytes 16900
  0.6 47.2 %copy-start = (f32[1408]{0:T(1024)S(1)}, f32[1408]{0:T(1024)}, u32[]{:S(2)}) copy-start(f32[1408]{0:T(1024)} %row_ref.1) | copy-start | bytes 16900

commit v3 on v2

--- a/solution.py
+++ b/solution.py
@@ -8,6 +8,8 @@
 from jax.sharding import PartitionSpec as P
 
 CHECK_COLS = 128
+SPLIT = 2
+LEAD, START, HOP = 1.5, 2.5, 1.7
 
 
 def for_sending(array):
@@ -146,12 +148,28 @@
     for load in loads:
         load.wait()
 
-    def cross(a):
-        return remote(src.at[a], crossed, cross_send, cross_recv, to_y)
+    width = w_ref.shape[1]
+    edges = [width // CHECK_COLS * h // SPLIT * CHECK_COLS for h in range(SPLIT)] + [width]
+    cuts = [pl.ds(low, high - low) for low, high in zip(edges, edges[1:])]
+
+    def own_at(a, k, h):
+        return own.at[a, k, :, cuts[h]]
+
+    def transit_at(a, k, h):
+        return transit.at[a - 1, k, :, cuts[h]]
+
+    def cross(a, h):
+        return remote(
+            src.at[a, :, cuts[h]],
+            crossed.at[:, cuts[h]],
+            cross_send.at[h],
+            cross_recv.at[h],
+            to_y,
+        )
 
     def z_copies(pos, turn, pieces, act):
-        for a, piece, slot, sem in pieces:
-            away = remote(piece, slot, z_send.at[turn, a], sem, to_z(pos))
+        for a, h, piece, slot, sem in pieces:
+            away = remote(piece, slot, z_send.at[turn, a, h], sem, to_z(pos))
             near = pltpu.make_async_copy(piece, slot, sem)
 
             @pl.when(pos != z)
@@ -168,46 +186,69 @@
                     near.start()
 
     mine, other = 2 * core + y, 2 * core + 1 - y
-    diag_mine = [(a, src.at[a], own.at[a, z], own_recv.at[a, z]) for a in (0, 1)]
-    diag_other = [(0, crossed, own.at[0, z], own_recv.at[0, z])]
-    off_mine = [(a - 1, src.at[a], transit.at[a - 1, z], transit_recv.at[a - 1, z]) for a in (1, 2)]
-    off_other = [(0, crossed, transit.at[1, z], transit_recv.at[1, z])]
-
-    @pl.when(diag)
-    def _():
-        cross(2).start()
-        z_copies(mine, 0, diag_mine, "start")
-        cross(2).wait_recv()
-        z_copies(other, 1, diag_other, "start")
-
-    @pl.when(jnp.logical_not(diag))
-    def _():
-        cross(0).start()
-        z_copies(mine, 0, off_mine, "start")
-        cross(0).wait_recv()
-        z_copies(other, 1, off_other, "start")
-
-    def arrived(a, k):
-        pltpu.make_async_copy(own.at[a, k], own.at[a, k], own_recv.at[a, k]).wait()
-
-    def passed(a, k):
-        slot = transit.at[a - 1, k]
-        pltpu.make_async_copy(slot, slot, transit_recv.at[a - 1, k]).wait()
-
-    def own_x(a, k):
-        return remote(own.at[a, k], own.at[a, k], x_send.at[a, k], own_recv.at[a, k], to_x)
-
-    def transit_x(a, k):
-        slot = transit.at[a - 1, k]
-        return remote(slot, slot, x_send.at[a - 1, k], transit_recv.at[a - 1, k], to_x)
-
-    def transit_y(a, k):
+    halves = range(len(cuts))
+
+    def to_own(h, arrays, pieces):
+        return [(n, h, p, own_at(a, z, h), own_recv.at[a, z, h]) for n, (a, p) in enumerate(zip(arrays, pieces))]
+
+    def to_transit(h, arrays, pieces):
+        return [
+            (n, h, p, transit_at(a, z, h), transit_recv.at[a - 1, z, h])
+            for n, (a, p) in enumerate(zip(arrays, pieces))
+        ]
+
+    def source(arrays, h):
+        return [src.at[a, :, cuts[h]] for a in arrays]
+
+    def mine_pieces(on_diag, h):
+        if on_diag:
+            return to_own(h, (0, 1), source((0, 1), h))
+        return to_transit(h, (1, 2), source((1, 2), h))
+
+    def other_pieces(on_diag, h):
+        place, a = (to_own, 0) if on_diag else (to_transit, 2)
+        return place(h, (a,), [crossed.at[:, cuts[h]]])
+
+    for on_diag in (True, False):
+
+        @pl.when(diag == on_diag)
+        def _():
+            sent = 2 if on_diag else 0
+            for h in halves:
+                cross(sent, h).start()
+            for h in halves:
+                z_copies(mine, 0, mine_pieces(on_diag, h), "start")
+            for h in halves:
+                cross(sent, h).wait_recv()
+                z_copies(other, 1, other_pieces(on_diag, h), "start")
+
+    def arrived(a, k, h):
+        pltpu.make_async_copy(own_at(a, k, h), own_at(a, k, h), own_recv.at[a, k, h]).wait()
+
+    def passed(a, k, h):
+        slot = transit_at(a, k, h)
+        pltpu.make_async_copy(slot, slot, transit_recv.at[a - 1, k, h]).wait()
+
+    def own_x(a, k, h):
+        slot = own_at(a, k, h)
+        return remote(slot, slot, x_send.at[a, k, h], own_recv.at[a, k, h], to_x)
+
+    def transit_x(a, k, h):
+        slot = transit_at(a, k, h)
+        return remote(slot, slot, x_send.at[a - 1, k, h], transit_recv.at[a - 1, k, h], to_x)
+
+    def transit_y(a, k, h):
         return remote(
-            transit.at[a - 1, k], own.at[a, k], y_send.at[a - 1, k], own_recv.at[a, k], to_y
+            transit_at(a, k, h),
+            own_at(a, k, h),
+            y_send.at[a - 1, k, h],
+            own_recv.at[a, k, h],
+            to_y,
         )
 
-    def across(a, k):
-        return remote(own.at[a, k], own.at[a, k], d_send.at[a, k], own_recv.at[a, k], to_core)
+    def across(a, k, h):
+        slot = own_at(a, k, h)
+        return remote(slot, slot, d_send.at[a, k, h], own_recv.at[a, k, h], to_core)
 
     half = count // 2
 
@@ -220,46 +261,45 @@
 
     match = z % 2 == y
 
+    def in_turn(arrays, start, lag):
+        turns = [(start + lag, a, 0) for a in arrays]
+        for a in arrays:
+            turns += [(start + lag + LEAD + len(turns) - len(arrays), a, s) for s in range(1, count)]
+        return turns
+
     def forward(on_diag, on_match):
         direct, passing, late = ((0, 1), (1, 2), (2,)) if on_match else ((0,), (2,), (1, 2))
-        for step in range(count + 2):
-            if step < count:
-                k = piece(step)
+        start = 0.0 if on_match else START
+        hop = HOP
+        turns = [(t, "direct", a, s) for t, a, s in in_turn(direct, start, 0.0 if on_diag else hop)]
+        turns += [(t, "pass", a, s) for t, a, s in in_turn(passing, start, hop if on_diag else 0.0)]
+        turns += [(t, "late", a, s) for t, a, s in in_turn(late, START - start, 2 * hop + 0.1)]
+        turns = [(t + 3 * h / SPLIT, way, a, step, h) for t, way, a, step in turns for h in halves]
+        for _, way, a, step, h in sorted(turns):
+            k = piece(step)
+            if way == "pass":
+                passed(a, k, h)
+                transit_y(a, k, h).start()
+                if not on_diag:
+                    transit_x(a, k, h).start()
+            else:
+                arrived(a, k, h)
+                if way == "direct" and on_diag:
+                    own_x(a, k, h).start()
+                across(a, k, h).start()
+
+        @pl.loop(0, count)
+        def _(k):
+            for h in halves:
+                for a in range(3):
+                    across(a, k, h).wait_send()
+                for a in passing:
+                    transit_y(a, k, h).wait_send()
+                    if not on_diag:
+                        transit_x(a, k, h).wait_send()
                 if on_diag:
                     for a in direct:
-                        arrived(a, k)
-                        own_x(a, k).start()
-                        across(a, k).start()
-                else:
-                    for a in passing:
-                        passed(a, k)
-                        transit_x(a, k).start()
-                        transit_y(a, k).start()
-            if 1 <= step <= count:
-                k = piece(step - 1)
-                if on_diag:
-                    for a in passing:
-                        passed(a, k)
-                        transit_y(a, k).start()
-                else:
-                    for a in direct:
-                        arrived(a, k)
-                        across(a, k).start()
-            if step >= 2:
-                k = piece(step - 2)
-                for a in late:
-                    arrived(a, k)
-                    across(a, k).start()
-        for k in range(count):
-            for a in range(3):
-                across(a, k).wait_send()
-            for a in passing:
-                transit_y(a, k).wait_send()
-                if not on_diag:
-                    transit_x(a, k).wait_send()
-            if on_diag:
-                for a in direct:
-                    own_x(a, k).wait_send()
+                        own_x(a, k, h).wait_send()
 
     for on_diag in (True, False):
         for on_match in (True, False):
@@ -270,21 +310,20 @@
 
     @pl.when(jnp.logical_not(active))
     def _():
-        for k in range(count):
+        @pl.loop(0, count)
+        def _(k):
             for a in range(3):
-                arrived(a, k)
-
-    @pl.when(diag)
-    def _():
-        cross(2).wait_send()
-        z_copies(mine, 0, diag_mine, "wait")
-        z_copies(other, 1, diag_other, "wait")
-
-    @pl.when(jnp.logical_not(diag))
-    def _():
-        cross(0).wait_send()
-        z_copies(mine, 0, off_mine, "wait")
-        z_copies(other, 1, off_other, "wait")
+                for h in halves:
+                    arrived(a, k, h)
+
+    for on_diag in (True, False):
+
+        @pl.when(diag == on_diag)
+        def _():
+            for h in halves:
+                cross(2 if on_diag else 0, h).wait_send()
+                z_copies(mine, 0, mine_pieces(on_diag, h), "wait")
+                z_copies(other, 1, other_pieces(on_diag, h), "wait")
 
 
 def finish(count, own, row_ref, col_ref, out0, out1, out2, check_ref, acc, out_sem):
@@ -342,14 +381,14 @@
             pltpu.VMEM((rows, width), weights.dtype),
             pltpu.VMEM((2, count, rows, width), weights.dtype),
             dma((3,)),
-            dma(()),
-            dma(()),
-            dma((2, 2)),
-            dma((3, count)),
-            dma((2, count)),
-            dma((2, count)),
-            dma((2, count)),
-            dma((3, count)),
+            dma((SPLIT,)),
+            dma((SPLIT,)),
+            dma((2, 2, SPLIT)),
+            dma((3, count, SPLIT)),
+            dma((2, count, SPLIT)),
+            dma((2, count, SPLIT)),
+            dma((2, count, SPLIT)),
+            dma((3, count, SPLIT)),
         ],
         compiler_params=pltpu.CompilerParams(
             collective_id=0, has_side_effects=True

time: 50.4 us -> 47 us (0.933)
  Pallas kernels: 49.6 us -> 46.2 us
    pallas_call x1, Pallas kernels: 47.2 us -> 43.8 us  [routed(): pl.pallas_call(functools.partial(route, count), out_shape=pltpu.VMEM((3,...]
where the time goes in v3:
time: 47 us; the launch traced here: 46.8 us
  Pallas kernels  46.2 us (98%)
  between operations  0.67 us (1%)
    pallas_call x1, Pallas kernels, routed(): pl.pallas_call(functools.partial(route, count), out_shape=pltpu.VMEM((3,...  43.8 us
    pallas_call x1, Pallas kernels, routed(): pl.pallas_call(functools.partial(finish, count), out_shape=(tile, tile, t...  2.38 us

profile of v3, /device:TPU:5, one launch (start us, length us, event | category | flops | bytes accessed | tf_op | source)
XLA Modules:
  0.0 46.8 jit_solution(1453804159219405623)
XLA Ops:
  0.6 0.0 copy-start.1
  0.6 0.0 copy-start
  0.7 43.8 %shard_map.84.own = bf16[3,4,88,1408]{3,2,1,0:T(8,128)(2,1)S(1)} custom-call(bf16[88,1408]{1,0:T(8,128)(2,1)} %w_ref.1, bf16[88,1408]{1,0:T(8,128)(2,1)} %m_ref.1, bf16[88,1408]{1,0:T(8,128)(2,1)} %v_ref.1), custom_call_target="tpu_custom_call" | custom-call | tf_op jit(solution)/shard_map/pallas_call | solution.py:374
  44.4 0.0 copy-done.1
  44.5 0.0 copy-done
  44.5 2.4 %shard_map.85 = (bf16[4,88,1408]{2,1,0:T(8,128)(2,1)}, bf16[4,88,1408]{2,1,0:T(8,128)(2,1)}, bf16[4,88,1408]{2,1,0:T(8,128)(2,1)}, f32[3,1,1,11]{3,2,1,0:T(1,128)}) custom-call(bf16[3,4,88,1408]{3,2,1,0:T(8,128)(2,1)S(1)} %shard_map.84.own, f32[1408]{0:T(1024)S(1)} %copy-done, f32[1408]{0:T(1024)S(1)} %copy-done.1), custom_call_target="tpu_custom_call" | custom-call | tf_op jit(solution)/shard_map/pallas_call | solution.py:397
Async XLA Ops:
  0.6 43.8 %copy-start.1 = (f32[1408]{0:T(1024)S(1)}, f32[1408]{0:T(1024)}, u32[]{:S(2)}) copy-start(f32[1408]{0:T(1024)} %col_ref.1) | copy-start | bytes 16900
  0.6 43.8 %copy-start = (f32[1408]{0:T(1024)S(1)}, f32[1408]{0:T(1024)}, u32[]{:S(2)}) copy-start(f32[1408]{0:T(1024)} %row_ref.1) | copy-start | bytes 16900
